TPU v7x, 32 devices: a whole 2x2x4 slice. The times are simulated.
32 devices in a mesh: rows: 4 (over z), tp: 4 (over y, x), unit: 2 (over core).
Axes of the slice: x: 2, y: 2, z: 4, core: 2. Of those that a mesh axis runs over, the one named last changes fastest.
Arguments:
- train_query: bfloat16 [4096, 2048], P(('unit', 'rows'), 'tp'), parts along dimension 0, may hold values from -0.125 to 0.125
- low_query: bfloat16 [4096, 64], P(('unit', 'rows')), parts along dimension 0, may hold values from -0.125 to 0.125
- high_query: bfloat16 [128, 2048], P('unit', 'tp'), parts along dimension 0, may hold values from -0.75 to 0.75
- train_key: bfloat16 [4096, 512], P(('unit', 'rows'), 'tp'), parts along dimension 0, may hold values from -0.125 to 0.125
- low_key: bfloat16 [4096, 64], P(('unit', 'rows')), parts along dimension 0, may hold values from -0.125 to 0.125
- high_key: bfloat16 [128, 512], P('unit', 'tp'), parts along dimension 0, may hold values from -0.75 to 0.75
- train_value: bfloat16 [4096, 512], P(('unit', 'rows'), 'tp'), parts along dimension 0, may hold values from -0.125 to 0.125
- low_value: bfloat16 [4096, 64], P(('unit', 'rows')), parts along dimension 0, may hold values from -0.125 to 0.125
- high_value: bfloat16 [128, 512], P('unit', 'tp'), parts along dimension 0, may hold values from -0.75 to 0.75
- norm_train: float32 [4096], P(('unit', 'rows', 'tp')), parts along dimension 0, may hold values from 0.25 to 1.75
- norm_step: float32 [4096], P(('unit', 'rows', 'tp')), parts along dimension 0, may hold values from -0.3 to 0.3
Outputs:
- final_query: bfloat16 [4096, 2048], P(('unit', 'tp')), parts along dimension 0
- final_key: bfloat16 [1024, 2048], P(('unit', 'tp')), parts along dimension 0
- final_value: bfloat16 [1024, 2048], P(('unit', 'tp')), parts along dimension 0
- serve_norm: bfloat16 [4096], P('unit'), parts along dimension 0
There are 2 independent parts, one for each index of `unit`. A program takes and returns all parts, laid end to end along the dimension named above; each array names one. Nothing has to cross between parts.
All inputs are finite; a program needn't handle non-finite values.
Results may differ from a plain program's by a relative error of at most 0.001.
Values may be sent and summed in bfloat16 or wider, within the bound.
A program may use at most 64 MiB of HBM per device.

v0:
```python
import functools

import jax
import jax.numpy as jnp
from jax import lax
from jax.experimental import pallas as pl
from jax.experimental.pallas import tpu as pltpu
from jax.sharding import PartitionSpec as P

mix_rate = 0.5
MESH = pl.DeviceIdType.MESH
LANES = 128


def kernel(
    n,
    peers,
    rows,
    *refs,
):
    (tq, lq, hq, tk, lk, hk, tv, lv, hv, norm_train, norm_step) = refs[:11]
    (oq, ok, ov, out_norm) = refs[11:15]
    held = refs[15:26]
    (gains, sums, in_sem, send_sem, recv_sem, peer_send, peer_recv) = refs[26:]
    outs = (oq, ok, ov)
    me, part = lax.axis_index("rows"), lax.axis_index("tp")
    right, left = lax.rem(me + 1, n), lax.rem(me + n - 1, n)
    has_right, has_left = me < n - 1, me > 0

    barrier = pltpu.get_barrier_semaphore()

    def greet(axis, index):
        pl.semaphore_signal(barrier, inc=1, device_id={axis: index}, device_id_type=MESH)

    loads = [
        pltpu.make_async_copy(source, target, in_sem.at[i])
        for i, (source, target) in enumerate(zip(refs[:11], held))
    ]

    @pl.when(has_right)
    def _():
        greet("rows", right)

    @pl.when(has_left)
    def _():
        greet("rows", left)

    for step in range(1, peers):
        greet("tp", lax.rem(part + step, peers))
    for i in (1, 2, 0, 4, 5, 3, 7, 8, 6, 9, 10):
        loads[i].start()

    pieces = []
    for which, out in enumerate(outs):
        height = out.shape[-2]
        width = LANES if height % LANES == 0 else height
        pieces += [(which, start, width) for start in range(0, height, width)]
    norm_piece = len(pieces)

    def view(c, k):
        if c == norm_piece:
            return gains.at[k]
        which, start, width = pieces[c]
        out = outs[which]
        if len(out.shape) == 3:
            return out.at[k, pl.ds(start, width), :]
        return out.at[pl.ds(start, width), pl.ds(pl.multiple_of(k * rows, rows), rows)]

    def hop(c, k, way):
        return pltpu.make_async_remote_copy(
            src_ref=view(c, k),
            dst_ref=view(c, k),
            send_sem=send_sem.at[way, k, c],
            recv_sem=recv_sem.at[k, c],
            device_id={"rows": left if way else right},
            device_id_type=MESH,
        )

    def both_ways(c):
        @pl.when(has_right)
        def _():
            hop(c, me, 0).start()

        @pl.when(has_left)
        def _():
            hop(c, me, 1).start()

    ready = set()

    def merge(c):
        which, start, width = pieces[c]
        train, low, high = held[3 * which : 3 * which + 3]
        if which not in ready:
            ready.add(which)
            for i in (1, 2, 0):
                loads[3 * which + i].wait()
        span = pl.ds(start, width)
        product = lax.dot_general(
            high[:, span], low[...], (((0,), (0,)), ((), ())), preferred_element_type=jnp.float32
        )
        result = train[:, span].T.astype(jnp.float32) + mix_rate * product
        view(c, me)[...] = result.astype(jnp.bfloat16)

    merge(0)
    merge(1)
    pl.semaphore_wait(
        barrier, peers - 1 + has_right.astype(jnp.int32) + has_left.astype(jnp.int32)
    )
    both_ways(0)
    for c in range(2, norm_piece):
        merge(c)
        both_ways(c - 1)
    loads[9].wait()
    loads[10].wait()
    gains[me, part] = held[9][...] + held[10][...]
    both_ways(norm_piece - 1)

    def to_peer(step):
        return pltpu.make_async_remote_copy(
            src_ref=gains.at[me, part],
            dst_ref=gains.at[me, part],
            send_sem=peer_send.at[step],
            recv_sem=peer_recv.at[step],
            device_id={"tp": lax.rem(part + step, peers)},
            device_id_type=MESH,
        )

    for step in range(1, peers):
        to_peer(step).start()
    for step in range(1, peers):
        to_peer(step).wait()
    both_ways(norm_piece)

    def pass_on(step, carry):
        for c in range(norm_piece + 1):

            @pl.when(me - step >= 0)
            def _():
                hop(c, me - step, 0).wait_recv()

                @pl.when(has_right)
                def _():
                    hop(c, me - step, 0).start()

            @pl.when(me + step < n)
            def _():
                hop(c, me + step, 1).wait_recv()

                @pl.when(has_left)
                def _():
                    hop(c, me + step, 1).start()

        return carry

    lax.fori_loop(1, n, pass_on, 0)
    for k in range(n):
        for t in range(peers):
            sums[k * peers + t : k * peers + t + 1, :] = gains[k, t]
    out_norm[...] = sums[...].astype(jnp.bfloat16)

    def sent(step, carry):
        for c in range(norm_piece + 1):

            @pl.when((me - step >= 0) & has_right)
            def _():
                hop(c, me - step, 0).wait_send()

            @pl.when((me + step < n) & has_left)
            def _():
                hop(c, me + step, 1).wait_send()

        return carry

    lax.fori_loop(0, n, sent, 0)


def settle(*refs):
    *arrays, sem = refs
    half = len(arrays) // 2
    copies = [
        pltpu.make_async_copy(source, target, sem.at[i])
        for i, (source, target) in enumerate(zip(arrays[:half], arrays[half:]))
    ]
    for copy in copies:
        copy.start()
    for copy in copies:
        copy.wait()


def solution(mesh):
    n, peers = mesh.shape["rows"], mesh.shape["tp"]

    def shards(tq, lq, hq, tk, lk, hk, tv, lv, hv, norm_train, norm_step):
        rows = tq.shape[0]
        whole_tiles = rows % LANES == 0
        trains = (tq, tk, tv)
        operands = (
            tq, lq.T, hq, tk, lk.T, hk, tv, lv.T, hv,
            norm_train.reshape(1, -1), norm_step.reshape(1, -1),
        )
        heights = [train.shape[1] for train in trains]
        shapes = [
            (height, n * rows) if whole_tiles else (n, height, rows) for height in heights
        ]
        pieces = 1 + sum(h // LANES if h % LANES == 0 else 1 for h in heights)
        width = norm_train.shape[0]
        place = pltpu.VMEM if whole_tiles else jax.ShapeDtypeStruct
        outs = pl.pallas_call(
            functools.partial(kernel, n, peers, rows),
            out_shape=[
                place(shape, jnp.bfloat16) for shape in (*shapes, (n * peers, width))
            ],
            in_specs=[pl.BlockSpec(memory_space=pl.ANY)] * len(operands),
            out_specs=[pl.BlockSpec(memory_space=pltpu.VMEM)] * 4,
            scratch_shapes=[pltpu.VMEM(x.shape, x.dtype) for x in operands]
            + [
                pltpu.VMEM((n, peers, 1, width), jnp.float32),
                pltpu.VMEM((n * peers, width), jnp.float32),
                pltpu.SemaphoreType.DMA((len(operands),)),
                pltpu.SemaphoreType.DMA((2, n, pieces)),
                pltpu.SemaphoreType.DMA((n, pieces)),
                pltpu.SemaphoreType.DMA((peers,)),
                pltpu.SemaphoreType.DMA((peers,)),
            ],
            compiler_params=pltpu.CompilerParams(collective_id=0, has_side_effects=True),
        )(*operands)
        if whole_tiles:
            *finals, norm = pl.pallas_call(
                settle,
                out_shape=[jax.ShapeDtypeStruct(out.shape, out.dtype) for out in outs],
                in_specs=[pl.BlockSpec(memory_space=pltpu.VMEM)] * len(outs),
                out_specs=[pl.BlockSpec(memory_space=pl.ANY)] * len(outs),
                scratch_shapes=[pltpu.SemaphoreType.DMA((len(outs),))],
                compiler_params=pltpu.CompilerParams(vmem_limit_bytes=8 * 1024 * 1024),
            )(*outs)
            return (*finals, norm.reshape(-1))
        finals = [
            out.transpose(1, 0, 2).reshape(height, n * rows)
            for out, height in zip(outs, heights)
        ]
        return (*finals, outs[3].reshape(-1))

    in_specs = (
        P(("unit", "rows"), "tp"),
        P(("unit", "rows"), None),
        P("unit", "tp"),
    ) * 3 + (P(("unit", "rows", "tp")),) * 2
    out_specs = (P(("unit", "tp"), None),) * 3 + (P("unit"),)
    return jax.shard_map(shards, mesh=mesh, in_specs=in_specs, out_specs=out_specs, check_vma=False)
```

profile of v0, /device:TPU:0, one launch (start us, length us, event | category | flops | bytes accessed | tf_op | source)
XLA Modules:
  0.0 60.0 jit_solution(858961011820611757)
XLA Ops:
  0.6 57.6 %shard_map.138 = (bf16[512,2048]{1,0:T(8,128)(2,1)S(1)}, bf16[128,2048]{1,0:T(8,128)(2,1)S(1)}, bf16[128,2048]{1,0:T(8,128)(2,1)S(1)}, bf16[16,128]{1,0:T(8,128)(2,1)S(1)}) custom-call(bf16[512,512]{1,0:T(8,128)(2,1)} %refs_0_.1, bf16[64,512]{1,0:T(8,128)(2,1)} %bitcast.6, bf16[64,512]{1,0:T(8,128)(2,1)} %refs_2_.1, bf16[512,128]{1,0:T(8,128)(2,1)} %refs_3_.1, ...), custom_call_target="tpu_custom_call" | custom-call | tf_op jit(solution)/shard_map/pallas_call | solution.py:208
  58.3 1.7 %shard_map.139 = (bf16[512,2048]{1,0:T(8,128)(2,1)}, bf16[128,2048]{1,0:T(8,128)(2,1)}, bf16[128,2048]{1,0:T(8,128)(2,1)}, bf16[16,128]{1,0:T(8,128)(2,1)}) custom-call(bf16[512,2048]{1,0:T(8,128)(2,1)S(1)} %get-tuple-element.12.refs_0_, bf16[128,2048]{1,0:T(8,128)(2,1)S(1)} %get-tuple-element.13.refs_1_, bf16[128,2048]{1,0:T(8,128)(2,1)S(1)} %get-tuple-element.14.refs_2_, ...), custom_call_target="tpu_custom_call" | custom-call | tf_op jit(solution)/shard_map/pallas_call | solution.py:228
where the time goes:
time: 60.1 us; the launch traced here: 60 us
  Pallas kernels  59.3 us (99%)
  between operations  0.64 us (1%)
    pallas_call x1, Pallas kernels, shards(): pl.pallas_call(functools.partial(kernel, n, peers, rows), out_shape=[plac...  57.6 us
    pallas_call x1, Pallas kernels, shards(): pl.pallas_call(settle, out_shape=[jax.ShapeDtypeStruct(out.shape, out.dty...  1.7 us

commit v1 on v0

v1 whole, which is shorter than its diff:
```python
import functools

import jax
import jax.numpy as jnp
from jax import lax
from jax.experimental import pallas as pl
from jax.experimental.pallas import tpu as pltpu
from jax.sharding import PartitionSpec as P

mix_rate = 0.5
MESH = pl.DeviceIdType.MESH
LANES = 128
ORDER = (1, 2, 0)


def plan(heights):
    units, row = [], 0
    for which in ORDER:
        height = heights[which]
        width = LANES if height % LANES == 0 else height
        for start in range(0, height, width):
            units.append((which, start, width, row))
            row += width
    edges = [unit[3] for unit in units] + [row]
    cuts = sorted({0, 1, 1 + -(-3 * (len(units) - 1) // 5), len(units)})
    spans = [(a, b, edges[a], edges[b] - edges[a]) for a, b in zip(cuts, cuts[1:])]
    return units, spans, row


def partners(peers, part):
    if peers & (peers - 1):
        return [[(lax.rem(part + step, peers), part, 1) for step in range(1, peers)]]
    rounds, size = [], 1
    while size < peers:
        low = lax.rem(part, 2 * size) < size
        rounds.append([(jnp.where(low, part + size, part - size), part - lax.rem(part, size), size)])
        size *= 2
    return rounds


def kernel(n, peers, rows, units, spans, *refs):
    (tq, lq, hq, tk, lk, hk, tv, lv, hv, norm_train, norm_step) = refs[:11]
    gathered, out_norm = refs[11:13]
    held = refs[13:24]
    (gains, sums, in_sem, send_sem, recv_sem, peer_send, peer_recv, ready) = refs[24:]
    me, part = lax.axis_index("rows"), lax.axis_index("tp")
    right, left = lax.rem(me + 1, n), lax.rem(me + n - 1, n)
    has_right, has_left = me < n - 1, me > 0
    rounds = partners(peers, part)
    greeted = sum(len(group) for group in rounds)

    barrier = pltpu.get_barrier_semaphore()

    def greet(axis, index):
        pl.semaphore_signal(barrier, inc=1, device_id={axis: index}, device_id_type=MESH)

    loads = [
        pltpu.make_async_copy(source, target, in_sem.at[i])
        for i, (source, target) in enumerate(zip(refs[:11], held))
    ]

    @pl.when(has_right)
    def _():
        greet("rows", right)

    for group in rounds:
        for whom, _, _ in group:
            greet("tp", whom)
    for which in ORDER:
        for i in (1, 2, 0):
            loads[3 * which + i].start()
        if which == ORDER[0]:
            loads[9].start()
            loads[10].start()

    last = len(spans)
    norm_piece = last - 1

    def view(c, k):
        if c == norm_piece:
            return gains.at[k]
        _, _, start, height = spans[min(c, last - 1)]
        if len(gathered.shape) == 3:
            return gathered.at[k, pl.ds(start, height), :]
        return gathered.at[pl.ds(start, height), pl.ds(pl.multiple_of(k * rows, rows), rows)]

    def hop(c, k, way):
        return pltpu.make_async_remote_copy(
            src_ref=view(c, k),
            dst_ref=view(c, k),
            send_sem=send_sem.at[way, k, c],
            recv_sem=recv_sem.at[k, c],
            device_id={"rows": left if way else right},
            device_id_type=MESH,
        )

    def send(c, way):
        @pl.when(has_left if way else has_right)
        def _():
            hop(c, me, way).start()

    loaded = set()

    def merge(u):
        which, start, width, row = units[u]
        train, low, high = held[3 * which : 3 * which + 3]
        if which not in loaded:
            loaded.add(which)
            for i in (1, 2, 0):
                loads[3 * which + i].wait()
        span = pl.ds(start, width)
        product = lax.dot_general(
            high[:, span], low[...], (((0,), (0,)), ((), ())), preferred_element_type=jnp.float32
        )
        result = train[:, span].T.astype(jnp.float32) + mix_rate * product
        if len(gathered.shape) == 3:
            target = gathered.at[me, pl.ds(row, width), :]
        else:
            target = gathered.at[pl.ds(row, width), pl.ds(pl.multiple_of(me * rows, rows), rows)]
        target[...] = result.astype(jnp.bfloat16)

    def merge_span(c):
        for u in range(spans[min(c, last - 1)][0], spans[min(c, last - 1)][1]):
            merge(u)

    bulk = [c for c in range(last + 1) if c != norm_piece]
    merge_span(bulk[0])
    loads[9].wait()
    loads[10].wait()
    gains[me, part] = held[9][...] + held[10][...]
    pl.semaphore_wait(barrier, greeted + has_left.astype(jnp.int32))

    @pl.when(has_left)
    def _():
        pl.semaphore_signal(ready, inc=1, device_id={"rows": left}, device_id_type=MESH)

    send(bulk[0], 1)
    for c in bulk[1:]:
        merge_span(c)
        if c < norm_piece:
            send(c, 1)

    @pl.when(has_right)
    def _():
        pl.semaphore_wait(ready, 1)

    for c in bulk:
        if c < norm_piece:
            send(c, 0)

    flight = 0
    for group in rounds:
        copies = []
        for whom, first, size in group:
            entries = gains.at[me, pl.ds(first, size)]
            copies.append(
                pltpu.make_async_remote_copy(
                    src_ref=entries,
                    dst_ref=entries,
                    send_sem=peer_send.at[flight],
                    recv_sem=peer_recv.at[flight],
                    device_id={"tp": whom},
                    device_id_type=MESH,
                )
            )
            flight += 1
        for copy in copies:
            copy.start()
        for copy in copies:
            copy.wait()
    for way in (1, 0):
        for c in (norm_piece, last):
            send(c, way)

    def pass_on(step, carry):
        for c in range(last + 1):

            @pl.when(me + step < n)
            def _():
                hop(c, me + step, 1).wait_recv()

                @pl.when(has_left)
                def _():
                    hop(c, me + step, 1).start()

            @pl.when(me - step >= 0)
            def _():
                hop(c, me - step, 0).wait_recv()

                @pl.when(has_right)
                def _():
                    hop(c, me - step, 0).start()

        return carry

    lax.fori_loop(1, n - 1, pass_on, 0)

    def arrive(c):
        if n > 1:

            @pl.when(me == 0)
            def _():
                hop(c, n - 1, 1).wait_recv()

            @pl.when(me == n - 1)
            def _():
                hop(c, 0, 0).wait_recv()

    for c in range(last):
        arrive(c)
    for k in range(n):
        for t in range(peers):
            sums[k * peers + t : k * peers + t + 1, :] = gains[k, t]
    out_norm[...] = sums[...].astype(jnp.bfloat16)

    def sent(step, carry):
        for c in range(last + 1):

            @pl.when((me - step >= 0) & has_right)
            def _():
                hop(c, me - step, 0).wait_send()

            @pl.when((me + step < n) & has_left)
            def _():
                hop(c, me + step, 1).wait_send()

        return carry

    lax.fori_loop(0, n, sent, 0)
    arrive(last)


def settle(places, gathered, norm, *refs):
    *outs, out_norm, sem = refs
    copies = [
        pltpu.make_async_copy(gathered.at[pl.ds(row, out.shape[0]), :], out, sem.at[i])
        for i, (row, out) in enumerate(zip(places, outs))
    ]
    copies.append(pltpu.make_async_copy(norm, out_norm, sem.at[len(outs)]))
    for copy in copies:
        copy.start()
    for copy in copies:
        copy.wait()


def solution(mesh):
    n, peers = mesh.shape["rows"], mesh.shape["tp"]

    def shards(tq, lq, hq, tk, lk, hk, tv, lv, hv, norm_train, norm_step):
        rows = tq.shape[0]
        whole_tiles = rows % LANES == 0
        operands = (
            tq, lq.T, hq, tk, lk.T, hk, tv, lv.T, hv,
            norm_train.reshape(1, -1), norm_step.reshape(1, -1),
        )
        heights = [train.shape[1] for train in (tq, tk, tv)]
        units, spans, total = plan(heights)
        places = [min(row for which, _, _, row in units if which == i) for i in range(3)]
        width = norm_train.shape[0]
        place = pltpu.VMEM if whole_tiles else jax.ShapeDtypeStruct
        shape = (total, n * rows) if whole_tiles else (n, total, rows)
        flights = max(1, peers - 1)
        gathered, norm = pl.pallas_call(
            functools.partial(kernel, n, peers, rows, units, spans),
            out_shape=[
                place(shape, jnp.bfloat16),
                place((n * peers, width), jnp.bfloat16),
            ],
            in_specs=[pl.BlockSpec(memory_space=pl.ANY)] * len(operands),
            out_specs=[pl.BlockSpec(memory_space=pltpu.VMEM)] * 2,
            scratch_shapes=[pltpu.VMEM(x.shape, x.dtype) for x in operands]
            + [
                pltpu.VMEM((n, peers, 1, width), jnp.float32),
                pltpu.VMEM((n * peers, width), jnp.float32),
                pltpu.SemaphoreType.DMA((len(operands),)),
                pltpu.SemaphoreType.DMA((2, n, len(spans) + 1)),
                pltpu.SemaphoreType.DMA((n, len(spans) + 1)),
                pltpu.SemaphoreType.DMA((flights,)),
                pltpu.SemaphoreType.DMA((flights,)),
                pltpu.SemaphoreType.REGULAR,
            ],
            compiler_params=pltpu.CompilerParams(collective_id=0, has_side_effects=True),
        )(*operands)
        if whole_tiles:
            *finals, norm = pl.pallas_call(
                functools.partial(settle, places),
                out_shape=[
                    jax.ShapeDtypeStruct((height, n * rows), jnp.bfloat16) for height in heights
                ]
                + [jax.ShapeDtypeStruct(norm.shape, norm.dtype)],
                in_specs=[pl.BlockSpec(memory_space=pltpu.VMEM)] * 2,
                out_specs=[pl.BlockSpec(memory_space=pl.ANY)] * 4,
                scratch_shapes=[pltpu.SemaphoreType.DMA((4,))],
                compiler_params=pltpu.CompilerParams(vmem_limit_bytes=8 * 1024 * 1024),
            )(gathered, norm)
            return (*finals, norm.reshape(-1))
        finals = [
            gathered[:, row : row + height, :].transpose(1, 0, 2).reshape(height, n * rows)
            for row, height in zip(places, heights)
        ]
        return (*finals, norm.reshape(-1))

    in_specs = (
        P(("unit", "rows"), "tp"),
        P(("unit", "rows"), None),
        P("unit", "tp"),
    ) * 3 + (P(("unit", "rows", "tp")),) * 2
    out_specs = (P(("unit", "tp"), None),) * 3 + (P("unit"),)
    return jax.shard_map(shards, mesh=mesh, in_specs=in_specs, out_specs=out_specs, check_vma=False)
```

time: 60.1 us -> 58.8 us (0.978)
  Pallas kernels: 59.3 us -> 58 us
    pallas_call x2, Pallas kernels: 59.3 us -> 58 us  [the longest x1 56.3 us: shards(): pl.pallas_call(functools.partial(kernel, n, peers, rows, units, spans), o...]
where the time goes in v1:
time: 58.8 us; the launch traced here: 58.6 us
  Pallas kernels  58 us (99%)
  between operations  0.64 us (1%)
    pallas_call x1, Pallas kernels, shards(): pl.pallas_call(functools.partial(kernel, n, peers, rows, units, spans), o...  56.3 us
    pallas_call x1, Pallas kernels, shards(): pl.pallas_call(functools.partial(settle, places), out_shape=[jax.ShapeDty...  1.69 us

profile of v1, /device:TPU:0, one launch (start us, length us, event | category | flops | bytes accessed | tf_op | source)
XLA Modules:
  0.0 58.6 jit_solution(9538919813194022051)
XLA Ops:
  0.6 56.3 %shard_map.138 = (bf16[768,2048]{1,0:T(8,128)(2,1)S(1)}, bf16[16,128]{1,0:T(8,128)(2,1)S(1)}) custom-call(bf16[512,512]{1,0:T(8,128)(2,1)} %refs_0_.1, bf16[64,512]{1,0:T(8,128)(2,1)} %bitcast.6, bf16[64,512]{1,0:T(8,128)(2,1)} %refs_2_.1, bf16[512,128]{1,0:T(8,128)(2,1)} %refs_3_.1, bf16[64,512]{1,0:T(8,128)(2,1)} %bitcast.7, bf16[64,128]{1,0:T(8,128)(2,1)} %refs_5_.1, ...), custom_call_target="tpu_custom_call" | custom-call | tf_op jit(solution)/shard_map/pallas_call | solution.py:263
  56.9 1.7 %shard_map.139 = (bf16[512,2048]{1,0:T(8,128)(2,1)}, bf16[128,2048]{1,0:T(8,128)(2,1)}, bf16[128,2048]{1,0:T(8,128)(2,1)}, bf16[16,128]{1,0:T(8,128)(2,1)}) custom-call(bf16[768,2048]{1,0:T(8,128)(2,1)S(1)} %get-tuple-element.10.gathered, bf16[16,128]{1,0:T(8,128)(2,1)S(1)} %get-tuple-element.11.norm), custom_call_target="tpu_custom_call" | custom-call | tf_op jit(solution)/shard_map/pallas_call | solution.py:285

commit v2 on v1

--- a/solution.py
+++ b/solution.py
@@ -22,8 +22,8 @@
             units.append((which, start, width, row))
             row += width
     edges = [unit[3] for unit in units] + [row]
-    cuts = sorted({0, 1, 1 + -(-3 * (len(units) - 1) // 5), len(units)})
-    spans = [(a, b, edges[a], edges[b] - edges[a]) for a, b in zip(cuts, cuts[1:])]
+    cut = sum(unit[0] != ORDER[-1] for unit in units)
+    spans = [(0, cut, 0, edges[cut]), (cut, len(units), edges[cut], row - edges[cut])]
     return units, spans, row
 
 
@@ -38,21 +38,23 @@
     return rounds
 
 
-def kernel(n, peers, rows, units, spans, *refs):
+def kernel(n, peers, rows, early, units, spans, *refs):
     (tq, lq, hq, tk, lk, hk, tv, lv, hv, norm_train, norm_step) = refs[:11]
     gathered, out_norm = refs[11:13]
     held = refs[13:24]
-    (gains, sums, in_sem, send_sem, recv_sem, peer_send, peer_recv, ready) = refs[24:]
-    me, part = lax.axis_index("rows"), lax.axis_index("tp")
+    (gains, sums, raw_train, raw_low) = refs[24:28]
+    (in_sem, send_sem, recv_sem, raw_sem, peer_send, peer_recv, signs) = refs[28:]
+    me, part, unit = lax.axis_index("rows"), lax.axis_index("tp"), lax.axis_index("unit")
     right, left = lax.rem(me + 1, n), lax.rem(me + n - 1, n)
     has_right, has_left = me < n - 1, me > 0
     rounds = partners(peers, part)
-    greeted = sum(len(group) for group in rounds)
+    flat = [whom for group in rounds for whom, _, _ in group]
+    told, known = 1, 1 + len(flat)
 
     barrier = pltpu.get_barrier_semaphore()
 
-    def greet(axis, index):
-        pl.semaphore_signal(barrier, inc=1, device_id={axis: index}, device_id_type=MESH)
+    def sign(sem, axis, index):
+        pl.semaphore_signal(sem, inc=1, device_id={axis: index}, device_id_type=MESH)
 
     loads = [
         pltpu.make_async_copy(source, target, in_sem.at[i])
@@ -61,45 +63,105 @@
 
     @pl.when(has_right)
     def _():
-        greet("rows", right)
-
-    for group in rounds:
-        for whom, _, _ in group:
-            greet("tp", whom)
-    for which in ORDER:
+        sign(barrier, "rows", right)
+
+    @pl.when(me == 0)
+    def _():
+        for whom in flat:
+            sign(barrier, "tp", whom)
+
+    for which in ORDER[:2]:
         for i in (1, 2, 0):
             loads[3 * which + i].start()
-        if which == ORDER[0]:
-            loads[9].start()
-            loads[10].start()
-
-    last = len(spans)
-    norm_piece = last - 1
-
-    def view(c, k):
-        if c == norm_piece:
+    pl.semaphore_wait(barrier, jnp.where(has_left, 1, len(flat)))
+
+    @pl.when(has_left)
+    def _():
+        sign(signs.at[0], "rows", left)
+
+    raws = [
+        pltpu.make_async_remote_copy(
+            src_ref=source,
+            dst_ref=target,
+            send_sem=raw_sem.at[i],
+            recv_sem=raw_sem.at[2 + i],
+            device_id={"rows": left},
+            device_id_type=MESH,
+        )
+        for i, (source, target) in enumerate(
+            [(tq.at[pl.ds(0, LANES), :], raw_train), (lq.at[:, pl.ds(0, LANES)], raw_low)]
+            if early
+            else []
+        )
+    ]
+
+    @pl.when(me == 1)
+    def _():
+        for raw in raws:
+            raw.start()
+
+    for i in (1, 2, 0, 9, 10):
+        loads[i].start()
+
+    FIRST, GAINS, SECOND = range(3)
+
+    def view(c, k, trimmed=False):
+        if c == GAINS:
             return gains.at[k]
-        _, _, start, height = spans[min(c, last - 1)]
+        _, _, start, height = spans[c // 2]
         if len(gathered.shape) == 3:
             return gathered.at[k, pl.ds(start, height), :]
-        return gathered.at[pl.ds(start, height), pl.ds(pl.multiple_of(k * rows, rows), rows)]
-
-    def hop(c, k, way):
+        skip = LANES if trimmed else 0
+        column = pl.multiple_of(k * rows + skip, LANES)
+        return gathered.at[pl.ds(start, height), pl.ds(column, rows - skip)]
+
+    def hop(c, k, way, trimmed=False):
+        slot = k - 1 if way else k
         return pltpu.make_async_remote_copy(
-            src_ref=view(c, k),
-            dst_ref=view(c, k),
+            src_ref=view(c, k, trimmed),
+            dst_ref=view(c, k, trimmed),
             send_sem=send_sem.at[way, k, c],
-            recv_sem=recv_sem.at[k, c],
+            recv_sem=recv_sem.at[slot, c],
             device_id={"rows": left if way else right},
             device_id_type=MESH,
         )
 
     def send(c, way):
-        @pl.when(has_left if way else has_right)
-        def _():
-            hop(c, me, way).start()
+        if not way:
+
+            @pl.when(has_right)
+            def _():
+                hop(c, me, 0).start()
+
+        elif early and c == SECOND:
+
+            @pl.when(me == 1)
+            def _():
+                hop(c, me, 1, True).start()
+
+            @pl.when(me > 1)
+            def _():
+                hop(c, me, 1).start()
+
+        else:
+
+            @pl.when(has_left)
+            def _():
+                hop(c, me, 1).start()
 
     loaded = set()
+
+    def put(row, width, k, skip, count, high, low, train):
+        product = lax.dot_general(
+            high, low, (((0,), (0,)), ((), ())), preferred_element_type=jnp.float32
+        )
+        result = train.T.astype(jnp.float32) + mix_rate * product
+        if len(gathered.shape) == 3:
+            target = gathered.at[k, pl.ds(row, width), :]
+        else:
+            column = pl.multiple_of(k * rows + skip, LANES)
+            target = gathered.at[pl.ds(row, width), pl.ds(column, count)]
+        target[...] = result.astype(jnp.bfloat16)
 
     def merge(u):
         which, start, width, row = units[u]
@@ -109,44 +171,46 @@
             for i in (1, 2, 0):
                 loads[3 * which + i].wait()
         span = pl.ds(start, width)
-        product = lax.dot_general(
-            high[:, span], low[...], (((0,), (0,)), ((), ())), preferred_element_type=jnp.float32
-        )
-        result = train[:, span].T.astype(jnp.float32) + mix_rate * product
-        if len(gathered.shape) == 3:
-            target = gathered.at[me, pl.ds(row, width), :]
-        else:
-            target = gathered.at[pl.ds(row, width), pl.ds(pl.multiple_of(me * rows, rows), rows)]
-        target[...] = result.astype(jnp.bfloat16)
+        put(row, width, me, 0, rows, high[:, span], low[...], train[:, span])
 
     def merge_span(c):
-        for u in range(spans[min(c, last - 1)][0], spans[min(c, last - 1)][1]):
+        for u in range(*spans[c // 2][:2]):
             merge(u)
 
-    bulk = [c for c in range(last + 1) if c != norm_piece]
-    merge_span(bulk[0])
+    merge_span(FIRST)
+    send(FIRST, 1)
+
+    @pl.when(has_right)
+    def _():
+        pl.semaphore_wait(signs.at[0], 1)
+
+    send(FIRST, 0)
+    merge_span(SECOND)
+
+    def send_second():
+        send(SECOND, 1)
+        send(SECOND, 0)
+
+    @pl.when(unit == 0)
+    def _():
+        send_second()
+
     loads[9].wait()
     loads[10].wait()
     gains[me, part] = held[9][...] + held[10][...]
-    pl.semaphore_wait(barrier, greeted + has_left.astype(jnp.int32))
 
     @pl.when(has_left)
     def _():
-        pl.semaphore_signal(ready, inc=1, device_id={"rows": left}, device_id_type=MESH)
-
-    send(bulk[0], 1)
-    for c in bulk[1:]:
-        merge_span(c)
-        if c < norm_piece:
-            send(c, 1)
+        for j in range(len(flat)):
+            pl.semaphore_wait(signs.at[known + j], 1)
 
     @pl.when(has_right)
     def _():
-        pl.semaphore_wait(ready, 1)
-
-    for c in bulk:
-        if c < norm_piece:
-            send(c, 0)
+        for j, whom in enumerate(flat):
+            sign(signs.at[told + j], "tp", whom)
+        for j in range(len(flat)):
+            pl.semaphore_wait(signs.at[told + j], 1)
+            sign(signs.at[known + j], "rows", right)
 
     flight = 0
     for group in rounds:
@@ -168,16 +232,33 @@
             copy.start()
         for copy in copies:
             copy.wait()
-    for way in (1, 0):
-        for c in (norm_piece, last):
-            send(c, way)
+    @pl.when(unit != 0)
+    def _():
+        send_second()
+
+    send(GAINS, 1)
+    send(GAINS, 0)
+
+    def take_left(c, step):
+        if early and c == SECOND and isinstance(step, int) and step == 1:
+
+            @pl.when(me == 0)
+            def _():
+                hop(c, me + step, 1, True).wait_recv()
+
+            @pl.when(me > 0)
+            def _():
+                hop(c, me + step, 1).wait_recv()
+
+        else:
+            hop(c, me + step, 1).wait_recv()
 
     def pass_on(step, carry):
-        for c in range(last + 1):
+        for c in range(3):
 
             @pl.when(me + step < n)
             def _():
-                hop(c, me + step, 1).wait_recv()
+                take_left(c, step)
 
                 @pl.when(has_left)
                 def _():
@@ -193,41 +274,75 @@
 
         return carry
 
-    lax.fori_loop(1, n - 1, pass_on, 0)
-
     def arrive(c):
         if n > 1:
 
             @pl.when(me == 0)
             def _():
-                hop(c, n - 1, 1).wait_recv()
+                take_left(c, n - 1)
 
             @pl.when(me == n - 1)
             def _():
                 hop(c, 0, 0).wait_recv()
 
-    for c in range(last):
-        arrive(c)
+    if n > 2:
+        pass_on(1, 0)
+        lax.fori_loop(2, n - 1, pass_on, 0)
+
+    @pl.when(me == 0)
+    def _():
+        for raw in raws:
+            raw.wait_recv()
+        for which, start, width, row in units if raws else []:
+            if which == 0:
+                span = pl.ds(start, width)
+                put(row, width, 1, 0, LANES, held[2][:, span], raw_low[...], raw_train[:, span])
+
+    arrive(FIRST)
+    arrive(GAINS)
     for k in range(n):
         for t in range(peers):
             sums[k * peers + t : k * peers + t + 1, :] = gains[k, t]
     out_norm[...] = sums[...].astype(jnp.bfloat16)
 
+    @pl.when(me == 1)
+    def _():
+        for raw in raws:
+            raw.wait_send()
+
+    def sent_left(c, step):
+        if early and c == SECOND and isinstance(step, int) and step == 0:
+
+            @pl.when(me == 1)
+            def _():
+                hop(c, me + step, 1, True).wait_send()
+
+            @pl.when(me > 1)
+            def _():
+                hop(c, me + step, 1).wait_send()
+
+        else:
+
+            @pl.when(has_left)
+            def _():
+                hop(c, me + step, 1).wait_send()
+
     def sent(step, carry):
-        for c in range(last + 1):
+        for c in range(3):
 
             @pl.when((me - step >= 0) & has_right)
             def _():
                 hop(c, me - step, 0).wait_send()
 
-            @pl.when((me + step < n) & has_left)
-            def _():
-                hop(c, me + step, 1).wait_send()
+            @pl.when(me + step < n)
+            def _():
+                sent_left(c, step)
 
         return carry
 
-    lax.fori_loop(0, n, sent, 0)
-    arrive(last)
+    sent(0, 0)
+    lax.fori_loop(1, n, sent, 0)
+    arrive(SECOND)
 
 
 def settle(places, gathered, norm, *refs):
@@ -259,9 +374,12 @@
         width = norm_train.shape[0]
         place = pltpu.VMEM if whole_tiles else jax.ShapeDtypeStruct
         shape = (total, n * rows) if whole_tiles else (n, total, rows)
-        flights = max(1, peers - 1)
+        rounds = partners(peers, 0)
+        flights = max(1, sum(len(group) for group in rounds))
+        early = n > 1 and whole_tiles and rows > LANES and heights[0] % LANES == 0
+        raw = LANES if early else rows
         gathered, norm = pl.pallas_call(
-            functools.partial(kernel, n, peers, rows, units, spans),
+            functools.partial(kernel, n, peers, rows, early, units, spans),
             out_shape=[
                 place(shape, jnp.bfloat16),
                 place((n * peers, width), jnp.bfloat16),
@@ -272,12 +390,15 @@
             + [
                 pltpu.VMEM((n, peers, 1, width), jnp.float32),
                 pltpu.VMEM((n * peers, width), jnp.float32),
+                pltpu.VMEM((raw, tq.shape[1]), tq.dtype),
+                pltpu.VMEM((lq.shape[1], raw), lq.dtype),
                 pltpu.SemaphoreType.DMA((len(operands),)),
-                pltpu.SemaphoreType.DMA((2, n, len(spans) + 1)),
-                pltpu.SemaphoreType.DMA((n, len(spans) + 1)),
+                pltpu.SemaphoreType.DMA((2, n, 3)),
+                pltpu.SemaphoreType.DMA((max(1, n - 1), 3)),
+                pltpu.SemaphoreType.DMA((4,)),
                 pltpu.SemaphoreType.DMA((flights,)),
                 pltpu.SemaphoreType.DMA((flights,)),
-                pltpu.SemaphoreType.REGULAR,
+                pltpu.SemaphoreType.REGULAR((1 + 2 * flights,)),
             ],
             compiler_params=pltpu.CompilerParams(collective_id=0, has_side_effects=True),
         )(*operands)

time: 58.8 us -> 57.6 us (0.980)
  Pallas kernels: 58 us -> 56.8 us
    pallas_call x1, Pallas kernels: 56.3 us -> 55.1 us  [shards(): pl.pallas_call(functools.partial(kernel, n, peers, rows, early, units, sp...]
where the time goes in v2:
time: 57.6 us; the launch traced here: 57.4 us
  Pallas kernels  56.8 us (99%)
  between operations  0.64 us (1%)
    pallas_call x1, Pallas kernels, shards(): pl.pallas_call(functools.partial(kernel, n, peers, rows, early, units, sp...  55.1 us
    pallas_call x1, Pallas kernels, shards(): pl.pallas_call(functools.partial(settle, places), out_shape=[jax.ShapeDty...  1.69 us

profile of v2, /device:TPU:0, one launch (start us, length us, event | category | flops | bytes accessed | tf_op | source)
XLA Modules:
  0.0 57.4 jit_solution(17210082902365164535)
XLA Ops:
  0.6 55.1 %shard_map.138 = (bf16[768,2048]{1,0:T(8,128)(2,1)S(1)}, bf16[16,128]{1,0:T(8,128)(2,1)S(1)}) custom-call(bf16[512,512]{1,0:T(8,128)(2,1)} %refs_0_.1, bf16[64,512]{1,0:T(8,128)(2,1)} %bitcast.6, bf16[64,512]{1,0:T(8,128)(2,1)} %refs_2_.1, bf16[512,128]{1,0:T(8,128)(2,1)} %refs_3_.1, bf16[64,512]{1,0:T(8,128)(2,1)} %bitcast.7, bf16[64,128]{1,0:T(8,128)(2,1)} %refs_5_.1, ...), custom_call_target="tpu_custom_call" | custom-call | tf_op jit(solution)/shard_map/pallas_call | solution.py:381
  55.8 1.7 %shard_map.139 = (bf16[512,2048]{1,0:T(8,128)(2,1)}, bf16[128,2048]{1,0:T(8,128)(2,1)}, bf16[128,2048]{1,0:T(8,128)(2,1)}, bf16[16,128]{1,0:T(8,128)(2,1)}) custom-call(bf16[768,2048]{1,0:T(8,128)(2,1)S(1)} %get-tuple-element.10.gathered, bf16[16,128]{1,0:T(8,128)(2,1)S(1)} %get-tuple-element.11.norm), custom_call_target="tpu_custom_call" | custom-call | tf_op jit(solution)/shard_map/pallas_call | solution.py:406

commit v3 on v2

--- a/solution.py
+++ b/solution.py
@@ -9,7 +9,7 @@
 
 mix_rate = 0.5
 MESH = pl.DeviceIdType.MESH
-LANES = 128
+LANES, SUBLANES = 128, 16
 ORDER = (1, 2, 0)
 
 
@@ -42,8 +42,9 @@
     (tq, lq, hq, tk, lk, hk, tv, lv, hv, norm_train, norm_step) = refs[:11]
     gathered, out_norm = refs[11:13]
     held = refs[13:24]
-    (gains, sums, raw_train, raw_low) = refs[24:28]
-    (in_sem, send_sem, recv_sem, raw_sem, peer_send, peer_recv, signs) = refs[28:]
+    (gains, sums, raw_train, raw_low, via) = refs[24:29]
+    (in_sem, send_sem, recv_sem, raw_sem, low_sem, share_sem, via_sem) = refs[29:36]
+    (peer_send, peer_recv, signs) = refs[36:]
     me, part, unit = lax.axis_index("rows"), lax.axis_index("tp"), lax.axis_index("unit")
     right, left = lax.rem(me + 1, n), lax.rem(me + n - 1, n)
     has_right, has_left = me < n - 1, me > 0
@@ -79,43 +80,80 @@
     def _():
         sign(signs.at[0], "rows", left)
 
-    raws = [
-        pltpu.make_async_remote_copy(
-            src_ref=source,
-            dst_ref=target,
-            send_sem=raw_sem.at[i],
-            recv_sem=raw_sem.at[2 + i],
+    def raw_down():
+        return pltpu.make_async_remote_copy(
+            src_ref=tq.at[pl.ds(0, raw_train.shape[0]), :],
+            dst_ref=raw_train,
+            send_sem=raw_sem.at[0],
+            recv_sem=raw_sem.at[1],
             device_id={"rows": left},
             device_id_type=MESH,
         )
-        for i, (source, target) in enumerate(
-            [(tq.at[pl.ds(0, LANES), :], raw_train), (lq.at[:, pl.ds(0, LANES)], raw_low)]
-            if early
-            else []
-        )
-    ]
-
-    @pl.when(me == 1)
-    def _():
-        for raw in raws:
-            raw.start()
+
+    half = raw_low.shape[0] // 2
+    carriers = (1, 2)
+
+    def low_down(j):
+        return pltpu.make_async_remote_copy(
+            src_ref=lq.at[pl.ds(j * half, half), pl.ds(0, LANES)],
+            dst_ref=raw_low.at[pl.ds(j * half, half), :],
+            send_sem=low_sem.at[0],
+            recv_sem=low_sem.at[1 + j],
+            device_id={"rows": left},
+            device_id_type=MESH,
+        )
+
+    def low_across(j, step):
+        return pltpu.make_async_remote_copy(
+            src_ref=raw_low.at[pl.ds(j * half, half), :],
+            dst_ref=raw_low.at[pl.ds(j * half, half), :],
+            send_sem=share_sem.at[step - 1],
+            recv_sem=low_sem.at[1 + j],
+            device_id={"tp": lax.rem(carriers[j] + step, peers)},
+            device_id_type=MESH,
+        )
+
+    def detour(j, leg):
+        rows_there = pl.ds(gathered.shape[0] - (2 - j) * SUBLANES, SUBLANES)
+        block = gathered.at[rows_there, pl.ds(rows + LANES, rows - LANES)]
+        return pltpu.make_async_remote_copy(
+            src_ref=(block, via, via)[leg],
+            dst_ref=(via, via, block)[leg],
+            send_sem=via_sem.at[j],
+            recv_sem=via_sem.at[2 + j],
+            device_id=({"tp": carriers[j]}, {"rows": left}, {"tp": 0})[leg],
+            device_id_type=MESH,
+        )
+
+    if early:
+
+        @pl.when(me == 1)
+        def _():
+            raw_down().start()
+
+            for j in range(2):
+
+                @pl.when(part == carriers[j])
+                def _():
+                    low_down(j).start()
 
     for i in (1, 2, 0, 9, 10):
         loads[i].start()
 
     FIRST, GAINS, SECOND = range(3)
 
-    def view(c, k, trimmed=False):
+    def view(c, k, trimmed=0):
         if c == GAINS:
             return gains.at[k]
         _, _, start, height = spans[c // 2]
         if len(gathered.shape) == 3:
             return gathered.at[k, pl.ds(start, height), :]
         skip = LANES if trimmed else 0
+        height -= 2 * SUBLANES if trimmed == 2 else 0
         column = pl.multiple_of(k * rows + skip, LANES)
         return gathered.at[pl.ds(start, height), pl.ds(column, rows - skip)]
 
-    def hop(c, k, way, trimmed=False):
+    def hop(c, k, way, trimmed=0):
         slot = k - 1 if way else k
         return pltpu.make_async_remote_copy(
             src_ref=view(c, k, trimmed),
@@ -135,9 +173,13 @@
 
         elif early and c == SECOND:
 
-            @pl.when(me == 1)
-            def _():
-                hop(c, me, 1, True).start()
+            @pl.when((me == 1) & (part == 0))
+            def _():
+                hop(c, me, 1, 2).start()
+
+            @pl.when((me == 1) & (part > 0))
+            def _():
+                hop(c, me, 1, 1).start()
 
             @pl.when(me > 1)
             def _():
@@ -236,15 +278,34 @@
     def _():
         send_second()
 
+    if early:
+
+        @pl.when(me == 1)
+        def _():
+            for j in range(2):
+
+                @pl.when(part == 0)
+                def _():
+                    detour(j, 0).start()
+
+                @pl.when(part == carriers[j])
+                def _():
+                    detour(j, 0).wait_recv()
+                    detour(j, 1).start()
+
     send(GAINS, 1)
     send(GAINS, 0)
 
     def take_left(c, step):
         if early and c == SECOND and isinstance(step, int) and step == 1:
 
-            @pl.when(me == 0)
-            def _():
-                hop(c, me + step, 1, True).wait_recv()
+            @pl.when((me == 0) & (part == 0))
+            def _():
+                hop(c, me + step, 1, 2).wait_recv()
+
+            @pl.when((me == 0) & (part > 0))
+            def _():
+                hop(c, me + step, 1, 1).wait_recv()
 
             @pl.when(me > 0)
             def _():
@@ -285,18 +346,50 @@
             def _():
                 hop(c, 0, 0).wait_recv()
 
-    if n > 2:
-        pass_on(1, 0)
-        lax.fori_loop(2, n - 1, pass_on, 0)
-
-    @pl.when(me == 0)
-    def _():
-        for raw in raws:
-            raw.wait_recv()
-        for which, start, width, row in units if raws else []:
+    def end_of_line():
+        for j in range(2):
+
+            @pl.when(part == carriers[j])
+            def _():
+                low_down(j).wait_recv()
+                for step in range(1, peers):
+                    low_across(j, step).start()
+                detour(j, 1).wait_recv()
+                detour(j, 2).start()
+
+        for j in range(2):
+
+            @pl.when(part != carriers[j])
+            def _():
+                low_across(j, 1).wait_recv()
+
+        raw_down().wait_recv()
+        for which, start, width, row in units:
             if which == 0:
                 span = pl.ds(start, width)
                 put(row, width, 1, 0, LANES, held[2][:, span], raw_low[...], raw_train[:, span])
+        for j in range(2):
+
+            @pl.when(part == 0)
+            def _():
+                detour(j, 2).wait_recv()
+
+            @pl.when(part == carriers[j])
+            def _():
+                detour(j, 2).wait_send()
+                for step in range(1, peers):
+                    low_across(j, step).wait_send()
+
+    if n > 2:
+        pass_on(1, 0)
+    if early:
+
+        @pl.when(me == 0)
+        def _():
+            end_of_line()
+
+    if n > 2:
+        lax.fori_loop(2, n - 1, pass_on, 0)
 
     arrive(FIRST)
     arrive(GAINS)
@@ -305,17 +398,32 @@
             sums[k * peers + t : k * peers + t + 1, :] = gains[k, t]
     out_norm[...] = sums[...].astype(jnp.bfloat16)
 
-    @pl.when(me == 1)
-    def _():
-        for raw in raws:
-            raw.wait_send()
+    if early:
+
+        @pl.when(me == 1)
+        def _():
+            raw_down().wait_send()
+            for j in range(2):
+
+                @pl.when(part == 0)
+                def _():
+                    detour(j, 0).wait_send()
+
+                @pl.when(part == carriers[j])
+                def _():
+                    low_down(j).wait_send()
+                    detour(j, 1).wait_send()
 
     def sent_left(c, step):
         if early and c == SECOND and isinstance(step, int) and step == 0:
 
-            @pl.when(me == 1)
-            def _():
-                hop(c, me + step, 1, True).wait_send()
+            @pl.when((me == 1) & (part == 0))
+            def _():
+                hop(c, me + step, 1, 2).wait_send()
+
+            @pl.when((me == 1) & (part > 0))
+            def _():
+                hop(c, me + step, 1, 1).wait_send()
 
             @pl.when(me > 1)
             def _():
@@ -376,7 +484,9 @@
         shape = (total, n * rows) if whole_tiles else (n, total, rows)
         rounds = partners(peers, 0)
         flights = max(1, sum(len(group) for group in rounds))
-        early = n > 1 and whole_tiles and rows > LANES and heights[0] % LANES == 0
+        rank = lq.shape[1]
+        early = n > 2 and peers > 2 and whole_tiles and rows > LANES
+        early = early and heights[0] % LANES == 0 and rank % (2 * SUBLANES) == 0
         raw = LANES if early else rows
         gathered, norm = pl.pallas_call(
             functools.partial(kernel, n, peers, rows, early, units, spans),
@@ -391,10 +501,14 @@
                 pltpu.VMEM((n, peers, 1, width), jnp.float32),
                 pltpu.VMEM((n * peers, width), jnp.float32),
                 pltpu.VMEM((raw, tq.shape[1]), tq.dtype),
-                pltpu.VMEM((lq.shape[1], raw), lq.dtype),
+                pltpu.VMEM((rank, raw), lq.dtype),
+                pltpu.VMEM((SUBLANES, rows - raw if early else rows), jnp.bfloat16),
                 pltpu.SemaphoreType.DMA((len(operands),)),
                 pltpu.SemaphoreType.DMA((2, n, 3)),
                 pltpu.SemaphoreType.DMA((max(1, n - 1), 3)),
+                pltpu.SemaphoreType.DMA((2,)),
+                pltpu.SemaphoreType.DMA((3,)),
+                pltpu.SemaphoreType.DMA((max(1, peers - 1),)),
                 pltpu.SemaphoreType.DMA((4,)),
                 pltpu.SemaphoreType.DMA((flights,)),
                 pltpu.SemaphoreType.DMA((flights,)),

time: 57.6 us -> 56.9 us (0.988)
  the two profiles are of different devices: /device:TPU:0 before, /device:TPU:3 now
where the time goes in v3:
time: 56.9 us; the launch traced here: 56.3 us
  Pallas kernels  55.7 us (98%)
  between operations  0.64 us (1%)
    pallas_call x1, Pallas kernels, shards(): pl.pallas_call(functools.partial(kernel, n, peers, rows, early, units, sp...  54 us
    pallas_call x1, Pallas kernels, shards(): pl.pallas_call(functools.partial(settle, places), out_shape=[jax.ShapeDty...  1.69 us

profile of v3, /device:TPU:3, one launch (start us, length us, event | category | flops | bytes accessed | tf_op | source)
XLA Modules:
  0.0 56.3 jit_solution(445331448331907960)
XLA Ops:
  0.6 54.0 %shard_map.138 = (bf16[768,2048]{1,0:T(8,128)(2,1)S(1)}, bf16[16,128]{1,0:T(8,128)(2,1)S(1)}) custom-call(bf16[512,512]{1,0:T(8,128)(2,1)} %refs_0_.1, bf16[64,512]{1,0:T(8,128)(2,1)} %bitcast.6, bf16[64,512]{1,0:T(8,128)(2,1)} %refs_2_.1, bf16[512,128]{1,0:T(8,128)(2,1)} %refs_3_.1, bf16[64,512]{1,0:T(8,128)(2,1)} %bitcast.7, bf16[64,128]{1,0:T(8,128)(2,1)} %refs_5_.1, ...), custom_call_target="tpu_custom_call" | custom-call | tf_op jit(solution)/shard_map/pallas_call | solution.py:491
  54.6 1.7 %shard_map.139 = (bf16[512,2048]{1,0:T(8,128)(2,1)}, bf16[128,2048]{1,0:T(8,128)(2,1)}, bf16[128,2048]{1,0:T(8,128)(2,1)}, bf16[16,128]{1,0:T(8,128)(2,1)}) custom-call(bf16[768,2048]{1,0:T(8,128)(2,1)S(1)} %get-tuple-element.10.gathered, bf16[16,128]{1,0:T(8,128)(2,1)S(1)} %get-tuple-element.11.norm), custom_call_target="tpu_custom_call" | custom-call | tf_op jit(solution)/shard_map/pallas_call | solution.py:520

commit v4 on v3

--- a/solution.py
+++ b/solution.py
@@ -1,4 +1,5 @@
 import functools
+import math
 
 import jax
 import jax.numpy as jnp
@@ -43,14 +44,14 @@
     gathered, out_norm = refs[11:13]
     held = refs[13:24]
     (gains, sums, raw_train, raw_low, via) = refs[24:29]
-    (in_sem, send_sem, recv_sem, raw_sem, low_sem, share_sem, via_sem) = refs[29:36]
-    (peer_send, peer_recv, signs) = refs[36:]
+    (in_sem, send_sem, recv_sem, extra_send, extra_recv, peer_recv, signs) = refs[29:]
     me, part, unit = lax.axis_index("rows"), lax.axis_index("tp"), lax.axis_index("unit")
     right, left = lax.rem(me + 1, n), lax.rem(me + n - 1, n)
     has_right, has_left = me < n - 1, me > 0
+    whole_tiles = len(gathered.shape) == 2
     rounds = partners(peers, part)
     flat = [whom for group in rounds for whom, _, _ in group]
-    told, known = 1, 1 + len(flat)
+    nearby, told, known = (signs.at[i] for i in range(3))
 
     barrier = pltpu.get_barrier_semaphore()
 
@@ -58,9 +59,21 @@
         pl.semaphore_signal(sem, inc=1, device_id={axis: index}, device_id_type=MESH)
 
     loads = [
-        pltpu.make_async_copy(source, target, in_sem.at[i])
+        pltpu.make_async_copy(source, target, in_sem.at[i // 3 if whole_tiles else i])
         for i, (source, target) in enumerate(zip(refs[:11], held))
     ]
+
+    def all_loaded(group):
+        if not whole_tiles:
+            for load in loads[3 * group : 3 * group + 3]:
+                load.wait()
+            return
+        if group == 3:
+            view = gains.at[0, pl.ds(0, 2)]
+        else:
+            size = sum(math.prod(x.shape) for x in held[3 * group : 3 * group + 3])
+            view = gathered.at[pl.ds(0, size // rows), pl.ds(0, rows)]
+        pltpu.make_async_copy(view, view, in_sem.at[group]).wait()
 
     @pl.when(has_right)
     def _():
@@ -78,14 +91,14 @@
 
     @pl.when(has_left)
     def _():
-        sign(signs.at[0], "rows", left)
+        sign(nearby, "rows", left)
 
     def raw_down():
         return pltpu.make_async_remote_copy(
             src_ref=tq.at[pl.ds(0, raw_train.shape[0]), :],
             dst_ref=raw_train,
-            send_sem=raw_sem.at[0],
-            recv_sem=raw_sem.at[1],
+            send_sem=extra_send.at[0],
+            recv_sem=extra_recv.at[0],
             device_id={"rows": left},
             device_id_type=MESH,
         )
@@ -97,8 +110,8 @@
         return pltpu.make_async_remote_copy(
             src_ref=lq.at[pl.ds(j * half, half), pl.ds(0, LANES)],
             dst_ref=raw_low.at[pl.ds(j * half, half), :],
-            send_sem=low_sem.at[0],
-            recv_sem=low_sem.at[1 + j],
+            send_sem=extra_send.at[1],
+            recv_sem=extra_recv.at[1 + j],
             device_id={"rows": left},
             device_id_type=MESH,
         )
@@ -107,8 +120,8 @@
         return pltpu.make_async_remote_copy(
             src_ref=raw_low.at[pl.ds(j * half, half), :],
             dst_ref=raw_low.at[pl.ds(j * half, half), :],
-            send_sem=share_sem.at[step - 1],
-            recv_sem=low_sem.at[1 + j],
+            send_sem=extra_send.at[step],
+            recv_sem=extra_recv.at[1 + j],
             device_id={"tp": lax.rem(carriers[j] + step, peers)},
             device_id_type=MESH,
         )
@@ -119,8 +132,8 @@
         return pltpu.make_async_remote_copy(
             src_ref=(block, via, via)[leg],
             dst_ref=(via, via, block)[leg],
-            send_sem=via_sem.at[j],
-            recv_sem=via_sem.at[2 + j],
+            send_sem=extra_send.at[(1 + j, 2, 0)[leg]],
+            recv_sem=extra_recv.at[3 + j],
             device_id=({"tp": carriers[j]}, {"rows": left}, {"tp": 0})[leg],
             device_id_type=MESH,
         )
@@ -158,7 +171,7 @@
         return pltpu.make_async_remote_copy(
             src_ref=view(c, k, trimmed),
             dst_ref=view(c, k, trimmed),
-            send_sem=send_sem.at[way, k, c],
+            send_sem=send_sem.at[way, c],
             recv_sem=recv_sem.at[slot, c],
             device_id={"rows": left if way else right},
             device_id_type=MESH,
@@ -210,8 +223,7 @@
         train, low, high = held[3 * which : 3 * which + 3]
         if which not in loaded:
             loaded.add(which)
-            for i in (1, 2, 0):
-                loads[3 * which + i].wait()
+            all_loaded(which)
         span = pl.ds(start, width)
         put(row, width, me, 0, rows, high[:, span], low[...], train[:, span])
 
@@ -224,7 +236,7 @@
 
     @pl.when(has_right)
     def _():
-        pl.semaphore_wait(signs.at[0], 1)
+        pl.semaphore_wait(nearby, 1)
 
     send(FIRST, 0)
     merge_span(SECOND)
@@ -237,33 +249,30 @@
     def _():
         send_second()
 
-    loads[9].wait()
-    loads[10].wait()
+    all_loaded(3)
     gains[me, part] = held[9][...] + held[10][...]
 
     @pl.when(has_left)
     def _():
-        for j in range(len(flat)):
-            pl.semaphore_wait(signs.at[known + j], 1)
+        pl.semaphore_wait(known, 1)
 
     @pl.when(has_right)
     def _():
-        for j, whom in enumerate(flat):
-            sign(signs.at[told + j], "tp", whom)
-        for j in range(len(flat)):
-            pl.semaphore_wait(signs.at[told + j], 1)
-            sign(signs.at[known + j], "rows", right)
+        for whom in flat:
+            sign(told, "tp", whom)
+        pl.semaphore_wait(told, len(flat))
+        sign(known, "rows", right)
 
     flight = 0
     for group in rounds:
         copies = []
-        for whom, first, size in group:
+        for i, (whom, first, size) in enumerate(group):
             entries = gains.at[me, pl.ds(first, size)]
             copies.append(
                 pltpu.make_async_remote_copy(
                     src_ref=entries,
                     dst_ref=entries,
-                    send_sem=peer_send.at[flight],
+                    send_sem=extra_send.at[3 + i],
                     recv_sem=peer_recv.at[flight],
                     device_id={"tp": whom},
                     device_id_type=MESH,
@@ -314,12 +323,34 @@
         else:
             hop(c, me + step, 1).wait_recv()
 
+    def sent_left(c, step):
+        if early and c == SECOND and isinstance(step, int) and step == 0:
+
+            @pl.when((me == 1) & (part == 0))
+            def _():
+                hop(c, me + step, 1, 2).wait_send()
+
+            @pl.when((me == 1) & (part > 0))
+            def _():
+                hop(c, me + step, 1, 1).wait_send()
+
+            @pl.when(me > 1)
+            def _():
+                hop(c, me + step, 1).wait_send()
+
+        else:
+
+            @pl.when(has_left)
+            def _():
+                hop(c, me + step, 1).wait_send()
+
     def pass_on(step, carry):
         for c in range(3):
 
             @pl.when(me + step < n)
             def _():
                 take_left(c, step)
+                sent_left(c, step - 1)
 
                 @pl.when(has_left)
                 def _():
@@ -331,6 +362,7 @@
 
                 @pl.when(has_right)
                 def _():
+                    hop(c, me - step + 1, 0).wait_send()
                     hop(c, me - step, 0).start()
 
         return carry
@@ -414,42 +446,24 @@
                     low_down(j).wait_send()
                     detour(j, 1).wait_send()
 
-    def sent_left(c, step):
-        if early and c == SECOND and isinstance(step, int) and step == 0:
-
-            @pl.when((me == 1) & (part == 0))
-            def _():
-                hop(c, me + step, 1, 2).wait_send()
-
-            @pl.when((me == 1) & (part > 0))
-            def _():
-                hop(c, me + step, 1, 1).wait_send()
-
-            @pl.when(me > 1)
-            def _():
-                hop(c, me + step, 1).wait_send()
-
-        else:
-
-            @pl.when(has_left)
-            def _():
-                hop(c, me + step, 1).wait_send()
-
-    def sent(step, carry):
-        for c in range(3):
-
-            @pl.when((me - step >= 0) & has_right)
-            def _():
-                hop(c, me - step, 0).wait_send()
-
-            @pl.when(me + step < n)
-            def _():
-                sent_left(c, step)
-
-        return carry
-
-    sent(0, 0)
-    lax.fori_loop(1, n, sent, 0)
+    for c in range(3):
+        if n > 1:
+
+            @pl.when((me == n - 1) & has_left)
+            def _():
+                hop(c, me, 1).wait_send()
+
+            @pl.when(me == 0)
+            def _():
+                hop(c, me, 0).wait_send()
+
+        if n > 2:
+
+            @pl.when(has_left & has_right)
+            def _():
+                hop(c, n - 1, 1).wait_send()
+                hop(c, 0, 0).wait_send()
+
     arrive(SECOND)
 
 
@@ -503,16 +517,13 @@
                 pltpu.VMEM((raw, tq.shape[1]), tq.dtype),
                 pltpu.VMEM((rank, raw), lq.dtype),
                 pltpu.VMEM((SUBLANES, rows - raw if early else rows), jnp.bfloat16),
-                pltpu.SemaphoreType.DMA((len(operands),)),
-                pltpu.SemaphoreType.DMA((2, n, 3)),
+                pltpu.SemaphoreType.DMA((4 if whole_tiles else len(operands),)),
+                pltpu.SemaphoreType.DMA((2, 3)),
                 pltpu.SemaphoreType.DMA((max(1, n - 1), 3)),
-                pltpu.SemaphoreType.DMA((2,)),
-                pltpu.SemaphoreType.DMA((3,)),
-                pltpu.SemaphoreType.DMA((max(1, peers - 1),)),
-                pltpu.SemaphoreType.DMA((4,)),
+                pltpu.SemaphoreType.DMA((max(4, peers, 3 + max(len(group) for group in rounds)),)),
+                pltpu.SemaphoreType.DMA((5,)),
                 pltpu.SemaphoreType.DMA((flights,)),
-                pltpu.SemaphoreType.DMA((flights,)),
-                pltpu.SemaphoreType.REGULAR((1 + 2 * flights,)),
+                pltpu.SemaphoreType.REGULAR((3,)),
             ],
             compiler_params=pltpu.CompilerParams(collective_id=0, has_side_effects=True),
         )(*operands)

time: 56.9 us -> 56.6 us (level)
  no operation moved by 1% of the time
where the time goes in v4:
time: 56.6 us; the launch traced here: 56 us
  Pallas kernels  55.4 us (98%)
  between operations  0.64 us (1%)
    pallas_call x1, Pallas kernels, shards(): pl.pallas_call(functools.partial(kernel, n, peers, rows, early, units, sp...  53.7 us
    pallas_call x1, Pallas kernels, shards(): pl.pallas_call(functools.partial(settle, places), out_shape=[jax.ShapeDty...  1.69 us

profile of v4, /device:TPU:3, one launch (start us, length us, event | category | flops | bytes accessed | tf_op | source)
XLA Modules:
  0.0 56.0 jit_solution(2985751042102009339)
XLA Ops:
  0.6 53.7 %shard_map.138 = (bf16[768,2048]{1,0:T(8,128)(2,1)S(1)}, bf16[16,128]{1,0:T(8,128)(2,1)S(1)}) custom-call(bf16[512,512]{1,0:T(8,128)(2,1)} %refs_0_.1, bf16[64,512]{1,0:T(8,128)(2,1)} %bitcast.6, bf16[64,512]{1,0:T(8,128)(2,1)} %refs_2_.1, bf16[512,128]{1,0:T(8,128)(2,1)} %refs_3_.1, bf16[64,512]{1,0:T(8,128)(2,1)} %bitcast.7, bf16[64,128]{1,0:T(8,128)(2,1)} %refs_5_.1, ...), custom_call_target="tpu_custom_call" | custom-call | tf_op jit(solution)/shard_map/pallas_call | solution.py:505
  54.3 1.7 %shard_map.139 = (bf16[512,2048]{1,0:T(8,128)(2,1)}, bf16[128,2048]{1,0:T(8,128)(2,1)}, bf16[128,2048]{1,0:T(8,128)(2,1)}, bf16[16,128]{1,0:T(8,128)(2,1)}) custom-call(bf16[768,2048]{1,0:T(8,128)(2,1)S(1)} %get-tuple-element.10.gathered, bf16[16,128]{1,0:T(8,128)(2,1)S(1)} %get-tuple-element.11.norm), custom_call_target="tpu_custom_call" | custom-call | tf_op jit(solution)/shard_map/pallas_call | solution.py:531

commit v5 on v4

--- a/solution.py
+++ b/solution.py
@@ -103,26 +103,25 @@
             device_id_type=MESH,
         )
 
-    half = raw_low.shape[0] // 2
-    carriers = (1, 2)
-
-    def low_down(j):
+    carriers, low_carrier = (1, 2), peers - 1
+
+    def low_down():
         return pltpu.make_async_remote_copy(
-            src_ref=lq.at[pl.ds(j * half, half), pl.ds(0, LANES)],
-            dst_ref=raw_low.at[pl.ds(j * half, half), :],
+            src_ref=lq.at[:, pl.ds(0, LANES)],
+            dst_ref=raw_low,
             send_sem=extra_send.at[1],
-            recv_sem=extra_recv.at[1 + j],
+            recv_sem=extra_recv.at[1],
             device_id={"rows": left},
             device_id_type=MESH,
         )
 
-    def low_across(j, step):
+    def low_across(step):
         return pltpu.make_async_remote_copy(
-            src_ref=raw_low.at[pl.ds(j * half, half), :],
-            dst_ref=raw_low.at[pl.ds(j * half, half), :],
+            src_ref=raw_low,
+            dst_ref=raw_low,
             send_sem=extra_send.at[step],
-            recv_sem=extra_recv.at[1 + j],
-            device_id={"tp": lax.rem(carriers[j] + step, peers)},
+            recv_sem=extra_recv.at[1],
+            device_id={"tp": (low_carrier + step) % peers},
             device_id_type=MESH,
         )
 
@@ -133,7 +132,7 @@
             src_ref=(block, via, via)[leg],
             dst_ref=(via, via, block)[leg],
             send_sem=extra_send.at[(1 + j, 2, 0)[leg]],
-            recv_sem=extra_recv.at[3 + j],
+            recv_sem=extra_recv.at[2 + j],
             device_id=({"tp": carriers[j]}, {"rows": left}, {"tp": 0})[leg],
             device_id_type=MESH,
         )
@@ -144,11 +143,9 @@
         def _():
             raw_down().start()
 
-            for j in range(2):
-
-                @pl.when(part == carriers[j])
-                def _():
-                    low_down(j).start()
+            @pl.when(part == low_carrier)
+            def _():
+                low_down().start()
 
     for i in (1, 2, 0, 9, 10):
         loads[i].start()
@@ -157,7 +154,7 @@
 
     def view(c, k, trimmed=0):
         if c == GAINS:
-            return gains.at[k]
+            return gains.at[k, part]
         _, _, start, height = spans[c // 2]
         if len(gathered.shape) == 3:
             return gathered.at[k, pl.ds(start, height), :]
@@ -231,15 +228,27 @@
         for u in range(*spans[c // 2][:2]):
             merge(u)
 
+    yields = (unit > 0) & (me == 1) if early else me < 0
     merge_span(FIRST)
-    send(FIRST, 1)
+
+    @pl.when(~yields)
+    def _():
+        send(FIRST, 1)
 
     @pl.when(has_right)
     def _():
         pl.semaphore_wait(nearby, 1)
 
     send(FIRST, 0)
+    all_loaded(3)
+    gains[me, part] = held[9][...] + held[10][...]
     merge_span(SECOND)
+
+    @pl.when(~yields)
+    def _():
+        send(GAINS, 1)
+
+    send(GAINS, 0)
 
     def send_second():
         send(SECOND, 1)
@@ -248,9 +257,6 @@
     @pl.when(unit == 0)
     def _():
         send_second()
-
-    all_loaded(3)
-    gains[me, part] = held[9][...] + held[10][...]
 
     @pl.when(has_left)
     def _():
@@ -263,11 +269,168 @@
         pl.semaphore_wait(told, len(flat))
         sign(known, "rows", right)
 
+    @pl.when(yields)
+    def _():
+        send(FIRST, 1)
+        send(GAINS, 1)
+
+    if early:
+
+        @pl.when(me == 1)
+        def _():
+            for j in range(2):
+
+                @pl.when(part == 0)
+                def _():
+                    detour(j, 0).start()
+
+                @pl.when(part == carriers[j])
+                def _():
+                    detour(j, 0).wait_recv()
+                    detour(j, 1).start()
+
+    def take_left(c, step):
+        if early and c == SECOND and isinstance(step, int) and step == 1:
+
+            @pl.when((me == 0) & (part == 0))
+            def _():
+                hop(c, me + step, 1, 2).wait_recv()
+
+            @pl.when((me == 0) & (part > 0))
+            def _():
+                hop(c, me + step, 1, 1).wait_recv()
+
+            @pl.when(me > 0)
+            def _():
+                hop(c, me + step, 1).wait_recv()
+
+        else:
+            hop(c, me + step, 1).wait_recv()
+
+    def sent_left(c, step):
+        if early and c == SECOND and isinstance(step, int) and step == 0:
+
+            @pl.when((me == 1) & (part == 0))
+            def _():
+                hop(c, me + step, 1, 2).wait_send()
+
+            @pl.when((me == 1) & (part > 0))
+            def _():
+                hop(c, me + step, 1, 1).wait_send()
+
+            @pl.when(me > 1)
+            def _():
+                hop(c, me + step, 1).wait_send()
+
+        else:
+
+            @pl.when(has_left)
+            def _():
+                hop(c, me + step, 1).wait_send()
+
+    def pass_on(step, carry):
+        for c in range(3):
+
+            @pl.when(me + step < n)
+            def _():
+                take_left(c, step)
+                sent_left(c, step - 1)
+
+                @pl.when(has_left)
+                def _():
+                    hop(c, me + step, 1).start()
+
+            @pl.when(me - step >= 0)
+            def _():
+                hop(c, me - step, 0).wait_recv()
+
+                @pl.when(has_right)
+                def _():
+                    hop(c, me - step + 1, 0).wait_send()
+                    hop(c, me - step, 0).start()
+
+            if isinstance(step, int) and c == FIRST:
+
+                @pl.when(unit > 0)
+                def _():
+                    send_second()
+
+        return carry
+
+    def arrive(c):
+        if n > 1:
+
+            @pl.when(me == 0)
+            def _():
+                take_left(c, n - 1)
+
+            @pl.when(me == n - 1)
+            def _():
+                hop(c, 0, 0).wait_recv()
+
+    def end_of_line():
+        @pl.when(part == low_carrier)
+        def _():
+            low_down().wait_recv()
+            for step in range(1, peers):
+                low_across(step).start()
+
+        for j in range(2):
+
+            @pl.when(part == carriers[j])
+            def _():
+                detour(j, 1).wait_recv()
+                detour(j, 2).start()
+
+        @pl.when(part != low_carrier)
+        def _():
+            low_across(1).wait_recv()
+
+        raw_down().wait_recv()
+        for which, start, width, row in units:
+            if which == 0:
+                span = pl.ds(start, width)
+                put(row, width, 1, 0, LANES, held[2][:, span], raw_low[...], raw_train[:, span])
+        for j in range(2):
+
+            @pl.when(part == 0)
+            def _():
+                detour(j, 2).wait_recv()
+
+            @pl.when(part == carriers[j])
+            def _():
+                detour(j, 2).wait_send()
+
+        @pl.when(part == low_carrier)
+        def _():
+            for step in range(1, peers):
+                low_across(step).wait_send()
+
+    if n > 2:
+        pass_on(1, 0)
+    else:
+
+        @pl.when(unit > 0)
+        def _():
+            send_second()
+
+    if early:
+
+        @pl.when(me == 0)
+        def _():
+            end_of_line()
+
+    if n > 2:
+        lax.fori_loop(2, n - 1, pass_on, 0)
+
+    arrive(FIRST)
+    arrive(GAINS)
+
     flight = 0
     for group in rounds:
         copies = []
         for i, (whom, first, size) in enumerate(group):
-            entries = gains.at[me, pl.ds(first, size)]
+            entries = gains.at[:, pl.ds(first, size)]
             copies.append(
                 pltpu.make_async_remote_copy(
                     src_ref=entries,
@@ -283,148 +446,6 @@
             copy.start()
         for copy in copies:
             copy.wait()
-    @pl.when(unit != 0)
-    def _():
-        send_second()
-
-    if early:
-
-        @pl.when(me == 1)
-        def _():
-            for j in range(2):
-
-                @pl.when(part == 0)
-                def _():
-                    detour(j, 0).start()
-
-                @pl.when(part == carriers[j])
-                def _():
-                    detour(j, 0).wait_recv()
-                    detour(j, 1).start()
-
-    send(GAINS, 1)
-    send(GAINS, 0)
-
-    def take_left(c, step):
-        if early and c == SECOND and isinstance(step, int) and step == 1:
-
-            @pl.when((me == 0) & (part == 0))
-            def _():
-                hop(c, me + step, 1, 2).wait_recv()
-
-            @pl.when((me == 0) & (part > 0))
-            def _():
-                hop(c, me + step, 1, 1).wait_recv()
-
-            @pl.when(me > 0)
-            def _():
-                hop(c, me + step, 1).wait_recv()
-
-        else:
-            hop(c, me + step, 1).wait_recv()
-
-    def sent_left(c, step):
-        if early and c == SECOND and isinstance(step, int) and step == 0:
-
-            @pl.when((me == 1) & (part == 0))
-            def _():
-                hop(c, me + step, 1, 2).wait_send()
-
-            @pl.when((me == 1) & (part > 0))
-            def _():
-                hop(c, me + step, 1, 1).wait_send()
-
-            @pl.when(me > 1)
-            def _():
-                hop(c, me + step, 1).wait_send()
-
-        else:
-
-            @pl.when(has_left)
-            def _():
-                hop(c, me + step, 1).wait_send()
-
-    def pass_on(step, carry):
-        for c in range(3):
-
-            @pl.when(me + step < n)
-            def _():
-                take_left(c, step)
-                sent_left(c, step - 1)
-
-                @pl.when(has_left)
-                def _():
-                    hop(c, me + step, 1).start()
-
-            @pl.when(me - step >= 0)
-            def _():
-                hop(c, me - step, 0).wait_recv()
-
-                @pl.when(has_right)
-                def _():
-                    hop(c, me - step + 1, 0).wait_send()
-                    hop(c, me - step, 0).start()
-
-        return carry
-
-    def arrive(c):
-        if n > 1:
-
-            @pl.when(me == 0)
-            def _():
-                take_left(c, n - 1)
-
-            @pl.when(me == n - 1)
-            def _():
-                hop(c, 0, 0).wait_recv()
-
-    def end_of_line():
-        for j in range(2):
-
-            @pl.when(part == carriers[j])
-            def _():
-                low_down(j).wait_recv()
-                for step in range(1, peers):
-                    low_across(j, step).start()
-                detour(j, 1).wait_recv()
-                detour(j, 2).start()
-
-        for j in range(2):
-
-            @pl.when(part != carriers[j])
-            def _():
-                low_across(j, 1).wait_recv()
-
-        raw_down().wait_recv()
-        for which, start, width, row in units:
-            if which == 0:
-                span = pl.ds(start, width)
-                put(row, width, 1, 0, LANES, held[2][:, span], raw_low[...], raw_train[:, span])
-        for j in range(2):
-
-            @pl.when(part == 0)
-            def _():
-                detour(j, 2).wait_recv()
-
-            @pl.when(part == carriers[j])
-            def _():
-                detour(j, 2).wait_send()
-                for step in range(1, peers):
-                    low_across(j, step).wait_send()
-
-    if n > 2:
-        pass_on(1, 0)
-    if early:
-
-        @pl.when(me == 0)
-        def _():
-            end_of_line()
-
-    if n > 2:
-        lax.fori_loop(2, n - 1, pass_on, 0)
-
-    arrive(FIRST)
-    arrive(GAINS)
     for k in range(n):
         for t in range(peers):
             sums[k * peers + t : k * peers + t + 1, :] = gains[k, t]
@@ -443,8 +464,11 @@
 
                 @pl.when(part == carriers[j])
                 def _():
-                    low_down(j).wait_send()
                     detour(j, 1).wait_send()
+
+            @pl.when(part == low_carrier)
+            def _():
+                low_down().wait_send()
 
     for c in range(3):
         if n > 1:
@@ -499,8 +523,8 @@
         rounds = partners(peers, 0)
         flights = max(1, sum(len(group) for group in rounds))
         rank = lq.shape[1]
-        early = n > 2 and peers > 2 and whole_tiles and rows > LANES
-        early = early and heights[0] % LANES == 0 and rank % (2 * SUBLANES) == 0
+        early = n > 2 and peers > 3 and whole_tiles and rows > LANES
+        early = early and heights[0] % LANES == 0
         raw = LANES if early else rows
         gathered, norm = pl.pallas_call(
             functools.partial(kernel, n, peers, rows, early, units, spans),
@@ -521,7 +545,7 @@
                 pltpu.SemaphoreType.DMA((2, 3)),
                 pltpu.SemaphoreType.DMA((max(1, n - 1), 3)),
                 pltpu.SemaphoreType.DMA((max(4, peers, 3 + max(len(group) for group in rounds)),)),
-                pltpu.SemaphoreType.DMA((5,)),
+                pltpu.SemaphoreType.DMA((4,)),
                 pltpu.SemaphoreType.DMA((flights,)),
                 pltpu.SemaphoreType.REGULAR((3,)),
             ],

time: 56.6 us -> 56.4 us (level)
  no operation moved by 1% of the time
where the time goes in v5:
time: 56.4 us; the launch traced here: 56.1 us
  Pallas kernels  55.5 us (98%)
  between operations  0.64 us (1%)
    pallas_call x1, Pallas kernels, shards(): pl.pallas_call(functools.partial(kernel, n, peers, rows, early, units, sp...  53.8 us
    pallas_call x1, Pallas kernels, shards(): pl.pallas_call(functools.partial(settle, places), out_shape=[jax.ShapeDty...  1.69 us

profile of v5, /device:TPU:3, one launch (start us, length us, event | category | flops | bytes accessed | tf_op | source)
XLA Modules:
  0.0 56.1 jit_solution(1399266640676711801)
XLA Ops:
  0.6 53.8 %shard_map.138 = (bf16[768,2048]{1,0:T(8,128)(2,1)S(1)}, bf16[16,128]{1,0:T(8,128)(2,1)S(1)}) custom-call(bf16[512,512]{1,0:T(8,128)(2,1)} %refs_0_.1, bf16[64,512]{1,0:T(8,128)(2,1)} %bitcast.6, bf16[64,512]{1,0:T(8,128)(2,1)} %refs_2_.1, bf16[512,128]{1,0:T(8,128)(2,1)} %refs_3_.1, bf16[64,512]{1,0:T(8,128)(2,1)} %bitcast.7, bf16[64,128]{1,0:T(8,128)(2,1)} %refs_5_.1, ...), custom_call_target="tpu_custom_call" | custom-call | tf_op jit(solution)/shard_map/pallas_call | solution.py:529
  54.4 1.7 %shard_map.139 = (bf16[512,2048]{1,0:T(8,128)(2,1)}, bf16[128,2048]{1,0:T(8,128)(2,1)}, bf16[128,2048]{1,0:T(8,128)(2,1)}, bf16[16,128]{1,0:T(8,128)(2,1)}) custom-call(bf16[768,2048]{1,0:T(8,128)(2,1)S(1)} %get-tuple-element.10.gathered, bf16[16,128]{1,0:T(8,128)(2,1)S(1)} %get-tuple-element.11.norm), custom_call_target="tpu_custom_call" | custom-call | tf_op jit(solution)/shard_map/pallas_call | solution.py:555
